TPU v7x, 128 devices: a whole 4x4x4 slice. The times are simulated.
128 devices in a mesh: aa: 4 (over x), ba: 4 (over z_hi, core), col: 8 (over y, z_lo).
Axes of the slice: x: 4, y: 4, z: 4 (z_hi: 2, z_lo: 2; z = z_hi * 2 + z_lo), core: 2. Of those that a mesh axis runs over, the one named last changes fastest.
Arguments:
- tokens: bfloat16 [64, 32, 64, 1024], P('aa', 'ba', 'col'), may hold values from -6 to 6
- norm_gain: float32 [1024], replicated, may hold values from 0.1 to 1.9
- in_weight: bfloat16 [1024, 3072], replicated, may hold values from -0.1875 to 0.1875
- skip_gain: float32 [1024], replicated, may hold values from 0.5 to 1.5
- spectrum_filter: bfloat16 [2, 64, 32, 64, 1024], P(None, ('ba', 'col'), None, None, 'aa'), may hold values from -4 to 4
- out_weight: bfloat16 [1024, 1024], replicated, may hold values from -0.1875 to 0.1875
Outputs:
- layer_out: bfloat16 [64, 32, 64, 1024], P('aa', 'ba', 'col')
All inputs are finite; a program needn't handle non-finite values.
Results may differ from a plain program's by a relative error of at most 0.014.
Values may be sent and summed in bfloat16 or wider, within the bound.
A program may use at most 128 MiB of HBM per device.

v0:
```python
import math

import jax
import jax.numpy as jnp
import numpy as np
from jax import lax
from jax.experimental import pallas as pl
from jax.experimental.pallas import tpu as pltpu
from jax.sharding import PartitionSpec as P

LA = 64
LB = 32
LC = 64
D = 1024
POINTS = LA * LB * LC
EPSILON = 1e-06
MESH = pl.DeviceIdType.MESH

NA, NB, NC = 4, 4, 8
SLOTS = NB * NC
NG = 4
NCC = 2
CHUNKS = NCC * NG
ROWS = 256
LANES = 128
HALF = LA // 2 + 1


def rounded(values):
    return np.asarray(values, np.float32).astype(jnp.bfloat16).astype(np.float32)


def dft_tables(length):
    counter = np.arange(length)
    angle = 2.0 * math.pi / length * (counter[:, None] * counter[None, :] % length)
    factor = 1.0 / math.sqrt(length)
    return rounded(np.cos(angle) * factor), rounded(np.sin(angle) * factor)


def static_tables():
    cos_a, sin_a = dft_tables(LA)
    small = np.zeros((HALF, 2, LA), np.float32)
    small[:, 0] = cos_a[:HALF]
    small[:, 1] = -sin_a[:HALF]
    small = small.reshape(HALF * 2, LA)
    table_a = np.repeat(small, 16, axis=1)
    table_lo = np.repeat(small[:LA].T, 16, axis=1)
    table_hi = np.repeat(small[2:].T, 16, axis=1)

    cos_b, sin_b = dft_tables(LB)
    lane = np.arange(512)
    j_of = 8 * (lane // 128) + 2 * (lane // 32 % 4) + lane // 8 % 2
    ri_of = lane // 16 % 2
    wc, ws = cos_b[:, j_of], sin_b[:, j_of]
    u2 = np.stack([np.where(ri_of, ws, wc), np.where(ri_of, wc, -ws)], 1).reshape(64, 512)
    v2 = np.stack([np.where(ri_of, wc, -ws), np.where(ri_of, -ws, -wc)], 1).reshape(64, 512)
    f0 = np.arange(LA)[:, None]
    sign = np.where((f0 >= LA // 2) & (ri_of[None] == 1), -1.0, 1.0)
    angle = 2.0 * math.pi / (LA * LB) * (f0 * j_of[None] % (LA * LB))
    cj, sj = np.cos(angle) * sign, np.sin(angle) * sign

    cos_c, sin_c = dft_tables(LC)
    lane = np.arange(128)
    k_of = 8 * (lane // 16) + lane % 8
    ri_of = lane // 8 % 2
    wc, ws = cos_c[:, k_of], sin_c[:, k_of]
    u3 = np.concatenate([np.where(ri_of, ws, wc), np.where(ri_of, wc, -ws)], 0)
    v3 = np.concatenate([np.where(ri_of, wc, -ws), np.where(ri_of, -ws, -wc)], 0)
    angle = 2.0 * math.pi / POINTS * (f0 * k_of[None] % POINTS)
    ca, sa = np.cos(angle), np.sin(angle)
    f1 = np.arange(LB)[:, None]
    angle = 2.0 * math.pi / (LB * LC) * (f1 * k_of[None] % (LB * LC))
    cb, sb = np.cos(angle), np.sin(angle)
    tables = (table_a, table_lo, table_hi, u2, v2, cj, sj, u3, v3, ca, sa, cb, sb)
    return tuple(np.asarray(t, np.float32) for t in tables)


def kernel(
    tok_hbm, gain_hbm, win_hbm, skip_hbm, filt_hbm, wout_hbm,
    ta_hbm, tlo_hbm, thi_hbm, u2_hbm, v2_hbm, cj_hbm, sj_hbm,
    u3_hbm, v3_hbm, ca_hbm, sa_hbm, cb_hbm, sb_hbm,
    out_hbm,
    tok, gain, wmix, wgate, skip, filt, wout,
    ta, tlo, thi, u2, v2, cj, sj, u3, v3, ca, sa, cb, sb,
    mixed, gate, xrecv, first, yzrecv, mid, mid2, bsend, brecv, csend, crecv, gated, outv,
    m1, mlo, mhi, t2, t2t, t3, t3t,
    lsem, osem, xs, xr, ys, yr, bs, br, cs, cr,
):
    a = lax.axis_index("aa")
    b = lax.axis_index("ba")
    c = lax.axis_index("col")
    s = b * NC + c

    loads = []

    def load(src, dst):
        copy = pltpu.make_async_copy(src, dst, lsem.at[len(loads)])
        copy.start()
        loads.append(copy)
        return copy

    first_loads = [load(gain_hbm, gain)]
    first_loads += [load(tok_hbm.at[:, pl.ds(16 * g, 16), :], tok.at[g]) for g in range(NG)]
    table_loads = [load(ta_hbm, ta), load(tlo_hbm, tlo), load(thi_hbm, thi)]
    mix_loads = []
    for cc in range(NCC):
        mix_loads.append([])
        for q in range(NA):
            for half, base in enumerate((0, 2 * D)):
                mix_loads[cc].append(
                    load(
                        win_hbm.at[:, pl.ds(base + 256 * q + 128 * cc, 128)],
                        wmix.at[cc, q, :, pl.ds(128 * half, 128)],
                    )
                )
    gate_loads = [load(win_hbm.at[:, pl.ds(D, D)], wgate)]
    late_loads = [
        load(src, dst)
        for src, dst in (
            (u2_hbm, u2), (v2_hbm, v2), (cj_hbm, cj), (sj_hbm, sj), (u3_hbm, u3), (v3_hbm, v3),
            (ca_hbm, ca), (sa_hbm, sa), (cb_hbm, cb), (sb_hbm, sb),
        )
    ]
    late_loads += [load(filt_hbm.at[..., pl.ds(128 * cc, 128)], filt.at[cc]) for cc in range(NCC)]
    end_loads = [load(skip_hbm, skip), load(wout_hbm, wout)]

    def x_device(d):
        return {"aa": lax.rem(a + d, NA), "ba": b, "col": c}

    def slot_of(d):
        return lax.rem(s + d, SLOTS)

    def yz_device(t):
        return {"aa": a, "ba": t // NC, "col": lax.rem(t, NC)}

    barrier = pltpu.get_barrier_semaphore()
    for d in range(1, NA):
        pl.semaphore_signal(barrier, inc=1, device_id=x_device(d), device_id_type=MESH)

    @pl.loop(1, SLOTS)
    def _(d):
        pl.semaphore_signal(barrier, inc=1, device_id=yz_device(slot_of(d)), device_id_type=MESH)

    for copy in table_loads:
        copy.wait()
    lane16 = lax.broadcasted_iota(jnp.int32, (16, 1024), 1)
    sub16 = lax.broadcasted_iota(jnp.int32, (16, 1024), 0)
    on16 = lax.rem(lane16, 16) == sub16

    @pl.loop(0, 2 * HALF)
    def _(r):
        m1[pl.ds(pl.multiple_of(16 * r, 16), 16), :] = jnp.where(on16, ta[pl.ds(r, 1), :], 0.0).astype(jnp.bfloat16)

    @pl.loop(0, LA)
    def _(r):
        at = pl.ds(pl.multiple_of(16 * r, 16), 16)
        mlo[at, :] = jnp.where(on16, tlo[pl.ds(r, 1), :], 0.0).astype(jnp.bfloat16)
        mhi[at, :] = jnp.where(on16, thi[pl.ds(r, 1), :], 0.0).astype(jnp.bfloat16)

    for copy in first_loads:
        copy.wait()

    @pl.loop(0, NG * 4)
    def _(n):
        g, part = n // 4, lax.rem(n, 4)
        view = tok.at[g, pl.ds(4 * part, 4)]
        block = view[...].astype(jnp.float32).reshape(64, D)
        scale = lax.rsqrt(jnp.mean(block * block, axis=-1, keepdims=True) + EPSILON)
        view[...] = (block * scale * gain[...]).astype(jnp.bfloat16).reshape(4, 16, D)

    pl.semaphore_wait(barrier, NA - 1 + SLOTS - 1)

    def x_copy(d, cc, g):
        to = lax.rem(a + d, NA)
        return pltpu.make_async_remote_copy(
            src_ref=mixed.at[to, cc, g], dst_ref=xrecv.at[cc, g, a],
            send_sem=xs.at[d, cc, g], recv_sem=xr.at[d, cc, g],
            device_id=x_device(d), device_id_type=MESH,
        )

    for cc in range(NCC):
        for copy in mix_loads[cc]:
            copy.wait()

        @pl.loop(0, NG)
        def _(g):
            rows = tok[g].reshape(ROWS, D)
            for q in range(NA):
                both = jnp.dot(rows, wmix[cc, q], preferred_element_type=jnp.float32)
                mixed[q, cc, g] = (both[:, :128] * both[:, 128:]).astype(jnp.bfloat16)
            for d in (2, 1, 3):
                x_copy(d, cc, g).start()
            xrecv[cc, g, a] = mixed[a, cc, g]

    def y_copy(d, cc, g):
        t = slot_of(d)
        p0 = jnp.where(t < SLOTS // 2, 2 * t, LA - 1 - 2 * t)
        return pltpu.make_async_remote_copy(
            src_ref=first.at[cc, g, pl.ds(p0, 2)], dst_ref=yzrecv.at[cc, :, c, b, g],
            send_sem=ys.at[d, cc, g], recv_sem=yr.at[d, cc, g],
            device_id=yz_device(t), device_id_type=MESH,
        )

    own0 = jnp.where(s < SLOTS // 2, 2 * s, LA - 1 - 2 * s)

    @pl.loop(0, CHUNKS)
    def _(n):
        cc, g = n // NG, lax.rem(n, NG)
        for d in (1, 3, 2):
            x_copy(d, cc, g).wait_recv()
        value = jnp.dot(m1[...], xrecv[cc, g].reshape(1024, LANES), preferred_element_type=jnp.float32)
        first[cc, g] = value.astype(jnp.bfloat16).reshape(HALF, 32, LANES)

        @pl.loop(1, SLOTS)
        def _(d):
            y_copy(d, cc, g).start()

        yzrecv[cc, :, c, b, g] = first[cc, g, pl.ds(own0, 2)]

    for copy in gate_loads:
        copy.wait()

    @pl.loop(0, NG)
    def _(g):
        value = jnp.dot(tok[g].reshape(ROWS, D), wgate[...], preferred_element_type=jnp.float32)
        gate[g] = value.astype(jnp.bfloat16)

    for copy in late_loads:
        copy.wait()
    lane8 = lax.broadcasted_iota(jnp.int32, (16, 512), 1)
    sub8 = lax.broadcasted_iota(jnp.int32, (16, 512), 0)
    on8 = lax.rem(lane8, 8) == lax.rem(sub8, 8)
    for u in range(2):
        f0 = jnp.where(s < SLOTS // 2, 2 * s + u, 2 * s + 1 - u)
        at0 = pl.ds(f0, 1)

        @pl.loop(0, LB)
        def _(f1):
            row0, row1 = pl.ds(2 * f1, 1), pl.ds(2 * f1 + 1, 1)
            up = u2[row0, :] * cj[at0, :] + v2[row0, :] * sj[at0, :]
            low = u2[row1, :] * cj[at0, :] + v2[row1, :] * sj[at0, :]
            value = jnp.where(on8, jnp.where(sub8 < 8, up, low), 0.0)
            t2[u, pl.ds(pl.multiple_of(16 * f1, 16), 16), :] = value.astype(jnp.bfloat16)

        @pl.loop(0, 4)
        def _(r):
            at = pl.ds(pl.multiple_of(128 * r, 128), 128)
            t2t[u, :, at] = jnp.transpose(t2[u, at, :].astype(jnp.float32)).astype(jnp.bfloat16)

        @pl.loop(0, LB)
        def _(f1):
            row = pl.ds(f1, 1)
            ec = ca[at0, :] * cb[row, :] - sa[at0, :] * sb[row, :]
            es = sa[at0, :] * cb[row, :] + ca[at0, :] * sb[row, :]
            value = u3[...] * ec + v3[...] * es
            t3[u, f1] = value.astype(jnp.bfloat16)
            t3t[u, f1] = jnp.transpose(value).astype(jnp.bfloat16)

    def b_copy(d, cc, g):
        t = slot_of(d)
        h = jnp.where(s < SLOTS // 2, 0, 1)
        q = jnp.where(s < SLOTS // 2, s, SLOTS - 1 - s)
        return pltpu.make_async_remote_copy(
            src_ref=bsend.at[cc, :, lax.rem(t, NC), t // NC, g], dst_ref=brecv.at[cc, g, h, q],
            send_sem=bs.at[d, cc, g], recv_sem=br.at[d, cc, g],
            device_id=yz_device(t), device_id_type=MESH,
        )

    own_h = jnp.where(s < SLOTS // 2, 0, 1)
    own_q = jnp.where(s < SLOTS // 2, s, SLOTS - 1 - s)

    @pl.loop(0, NCC)
    def _(cc):
        @pl.loop(1, SLOTS)
        def _(d):
            for g in range(NG):
                y_copy(d, cc, g).wait_recv()

        @pl.loop(0, 2)
        def _(u):
            l = jnp.where(s < SLOTS // 2, u, 1 - u)

            @pl.loop(0, NC // 2)
            def _(n):
                pair = [yzrecv[cc, u, 2 * n + m].reshape(512, LANES) for m in range(2)]
                value = jnp.dot(t2[u], jnp.concatenate(pair, axis=1), preferred_element_type=jnp.float32)
                value = value.astype(jnp.bfloat16)
                for m in range(2):
                    mid[:, 2 * n + m] = value[:, 128 * m : 128 * (m + 1)].reshape(LB, 16, LANES)

            @pl.loop(0, LB // 4)
            def _(n):
                spectra = []
                for e in range(4):
                    f1 = 4 * n + e
                    spectra.append(
                        jnp.dot(t3[u, f1], mid[f1].reshape(128, LANES), preferred_element_type=jnp.float32)
                    )
                outs = []
                for e in range(4):
                    f1 = 4 * n + e
                    xr_, xi_ = spectra[e][:64], spectra[e][64:]
                    hr = filt[cc, 0, l, f1].astype(jnp.float32)
                    hi = filt[cc, 1, l, f1].astype(jnp.float32)
                    outs.append(
                        jnp.concatenate([hr * xr_ - hi * xi_, hr * xi_ + hi * xr_], axis=0).astype(jnp.bfloat16)
                    )
                for e in range(4):
                    f1 = 4 * n + e
                    value = jnp.dot(t3t[u, f1], outs[e], preferred_element_type=jnp.float32)
                    mid2[f1] = value.astype(jnp.bfloat16).reshape(NC, 16, LANES)

            @pl.loop(0, NC // 2)
            def _(n):
                pair = [mid2[:, 2 * n + m].reshape(512, LANES) for m in range(2)]
                value = jnp.dot(t2t[u], jnp.concatenate(pair, axis=1), preferred_element_type=jnp.float32)
                value = value.astype(jnp.bfloat16)
                for m in range(2):
                    bsend[cc, u, 2 * n + m] = value[:, 128 * m : 128 * (m + 1)].reshape(NB, NG, 32, LANES)

        @pl.loop(0, NG)
        def _(g):
            @pl.loop(1, SLOTS)
            def _(d):
                b_copy(d, cc, g).start()

            brecv[cc, g, own_h, own_q] = bsend[cc, :, c, b, g]

    def c_copy(d, cc, g):
        to = lax.rem(a + d, NA)
        return pltpu.make_async_remote_copy(
            src_ref=csend.at[cc, g, to], dst_ref=crecv.at[cc, g, a],
            send_sem=cs.at[d, cc, g], recv_sem=cr.at[d, cc, g],
            device_id=x_device(d), device_id_type=MESH,
        )

    for copy in end_loads:
        copy.wait()

    @pl.loop(0, CHUNKS)
    def _(n):
        cc, g = n // NG, lax.rem(n, NG)

        @pl.loop(1, SLOTS)
        def _(d):
            b_copy(d, cc, g).wait_recv()

        value = jnp.dot(mlo[...], brecv[cc, g, 0].reshape(1024, LANES), preferred_element_type=jnp.float32)
        value += jnp.dot(mhi[...], brecv[cc, g, 1].reshape(1024, LANES), preferred_element_type=jnp.float32)
        csend[cc, g] = value.astype(jnp.bfloat16).reshape(NA, ROWS, LANES)
        for d in (2, 1, 3):
            c_copy(d, cc, g).start()
        crecv[cc, g, a] = csend[cc, g, a]

    def out_copy(g):
        return pltpu.make_async_copy(outv.at[g], out_hbm.at[:, pl.ds(16 * g, 16), :], osem.at[g])

    for g in range(NG):
        for cc in range(NCC):
            for d in (1, 3, 2):
                c_copy(d, cc, g).wait_recv()
        for q in range(NA):
            for cc in range(NCC):
                at = pl.ds(256 * q + 128 * cc, 128)
                conv = crecv[cc, g, q].astype(jnp.float32)
                plus = conv + skip[:, at] * mixed[q, cc, g].astype(jnp.float32)
                gated[:, at] = (gate[g, :, at].astype(jnp.float32) * plus).astype(jnp.bfloat16)
        value = jnp.dot(gated[...], wout[...], preferred_element_type=jnp.float32)
        outv[g] = value.astype(jnp.bfloat16).reshape(16, 16, D)
        out_copy(g).start()

    @pl.loop(0, CHUNKS)
    def _(n):
        cc, g = n // NG, lax.rem(n, NG)
        for d in range(1, NA):
            x_copy(d, cc, g).wait_send()
            c_copy(d, cc, g).wait_send()

        @pl.loop(1, SLOTS)
        def _(d):
            y_copy(d, cc, g).wait_send()
            b_copy(d, cc, g).wait_send()

    for g in range(NG):
        out_copy(g).wait()


def local(tokens, norm_gain, in_weight, skip_gain, spectrum_filter, out_weight):
    tables = [jnp.asarray(t) for t in static_tables()]
    bf, f32 = jnp.bfloat16, jnp.float32
    vmem = pltpu.VMEM
    dma = pltpu.SemaphoreType.DMA
    scratch = [
        vmem((NG, 16, 16, D), bf), vmem((1, D), f32), vmem((NCC, NA, D, 256), bf), vmem((D, D), bf),
        vmem((1, D), f32), vmem((NCC, 2, 2, LB, LC, LANES), bf), vmem((D, D), bf),
        *[vmem(t.shape, f32) for t in tables],
        vmem((NA, NCC, NG, ROWS, LANES), bf),
        vmem((NG, ROWS, D), bf),
        vmem((NCC, NG, NA, ROWS, LANES), bf),
        vmem((NCC, NG, HALF, 32, LANES), bf),
        vmem((NCC, 2, NC, NB, NG, 32, LANES), bf),
        vmem((LB, NC, 16, LANES), bf),
        vmem((LB, NC, 16, LANES), bf),
        vmem((NCC, 2, NC, NB, NG, 32, LANES), bf),
        vmem((NCC, NG, 2, 16, 2, 32, LANES), bf),
        vmem((NCC, NG, NA, ROWS, LANES), bf),
        vmem((NCC, NG, NA, ROWS, LANES), bf),
        vmem((ROWS, D), bf),
        vmem((NG, 16, 16, D), bf),
        vmem((HALF * 32, 1024), bf), vmem((1024, 1024), bf), vmem((1024, 1024), bf),
        vmem((2, 512, 512), bf), vmem((2, 512, 512), bf),
        vmem((2, LB, 128, 128), bf), vmem((2, LB, 128, 128), bf),
        dma((40,)), dma((NG,)),
        dma((NA, NCC, NG)), dma((NA, NCC, NG)),
        dma((SLOTS, NCC, NG)), dma((SLOTS, NCC, NG)),
        dma((SLOTS, NCC, NG)), dma((SLOTS, NCC, NG)),
        dma((NA, NCC, NG)), dma((NA, NCC, NG)),
    ]
    out = pl.pallas_call(
        kernel,
        out_shape=jax.ShapeDtypeStruct((16, 64, D), bf),
        in_specs=[pl.BlockSpec(memory_space=pl.ANY)] * (6 + len(tables)),
        out_specs=pl.BlockSpec(memory_space=pl.ANY),
        scratch_shapes=scratch,
        compiler_params=pltpu.CompilerParams(
            collective_id=0, has_side_effects=True, vmem_limit_bytes=67043328
        ),
    )(
        tokens.reshape(16, 64, D), norm_gain.reshape(1, D), in_weight, skip_gain.reshape(1, D),
        spectrum_filter, out_weight, *tables,
    )
    return out.reshape(16, 8, 8, D)


def solution(mesh):
    in_specs = (
        P("aa", "ba", "col", None),
        P(),
        P(),
        P(),
        P(None, ("ba", "col"), None, None, "aa"),
        P(),
    )
    out_specs = P("aa", "ba", "col", None)
    return jax.shard_map(local, mesh=mesh, in_specs=in_specs, out_specs=out_specs, check_vma=False)
```

profile of v0, /device:TPU:1, one launch (start us, length us, event | category | flops | bytes accessed | tf_op | source)
XLA Modules:
  0.0 145.8 jit_solution(12914814190211688502)
XLA Ops:
  0.0 142.6 %shard_map.181 = bf16[16,64,1024]{2,1,0:T(8,128)(2,1)} custom-call(bf16[16,64,1024]{2,1,0:T(8,128)(2,1)} %bitcast.5, f32[1,1024]{1,0:T(1,128)} %bitcast.6, bf16[1024,3072]{1,0:T(8,128)(2,1)} %win_hbm.1, f32[1,1024]{1,0:T(1,128)} %bitcast.7, bf16[2,2,32,64,256]{4,3,2,1,0:T(8,128)(2,1)} %filt_hbm.1, bf16[1024,1024]{1,0:T(8,128)(2,1)} %wout_hbm.1, ...), custom_call_target="tpu_custom_call" | custom-call | tf_op jit(solution)/shard_map/pallas_call | solution.py:419
  142.6 3.1 %copy.21 = bf16[16,8,8,1024]{3,2,1,0:T(8,128)(2,1)} copy(bf16[16,8,8,1024]{3,2,1,0:T(8,128)(2,1)} %bitcast.4) | data formatting | bytes 4194304
where the time goes:
time: 146 us
  Pallas kernels  143 us (98%)
  local copies, waits for them, and re-layouts  3.14 us (2%)
    pallas_call x1, Pallas kernels, local(): pl.pallas_call(kernel, out_shape=jax.ShapeDtypeStruct((16, 64, D), bf), i...  143 us
    unnamed x1, local copies, waits for them, and re-layouts  3.14 us

commit v1 on v0

v1 whole, which is shorter than its diff:
```python
import math

import jax
import jax.numpy as jnp
import numpy as np
from jax import lax
from jax.experimental import pallas as pl
from jax.experimental.pallas import tpu as pltpu
from jax.sharding import PartitionSpec as P

LA = 64
LB = 32
LC = 64
D = 1024
POINTS = LA * LB * LC
EPSILON = 1e-06
MESH = pl.DeviceIdType.MESH

NA, NB, NC = 4, 4, 8
SLOTS = NB * NC
NG = 4
NCC = 2
CHUNKS = NCC * NG
ROWS = 256
LANES = 128
HALF = LA // 2 + 1


def rounded(values):
    return np.asarray(values, np.float32).astype(jnp.bfloat16).astype(np.float32)


def dft_tables(length):
    counter = np.arange(length)
    angle = 2.0 * math.pi / length * (counter[:, None] * counter[None, :] % length)
    factor = 1.0 / math.sqrt(length)
    return rounded(np.cos(angle) * factor), rounded(np.sin(angle) * factor)


def static_tables():
    cos_a, sin_a = dft_tables(LA)
    small = np.zeros((HALF, 2, LA), np.float32)
    small[:, 0] = cos_a[:HALF]
    small[:, 1] = -sin_a[:HALF]
    small = small.reshape(HALF * 2, LA)
    table_a = np.repeat(small, 16, axis=1)
    table_lo = np.repeat(small[:LA].T, 16, axis=1)
    table_hi = np.repeat(small[2:].T, 16, axis=1)

    cos_b, sin_b = dft_tables(LB)
    lane = np.arange(512)
    j_of = 8 * (lane // 128) + 2 * (lane // 32 % 4) + lane // 8 % 2
    ri_of = lane // 16 % 2
    wc, ws = cos_b[:, j_of], sin_b[:, j_of]
    u2 = np.stack([np.where(ri_of, ws, wc), np.where(ri_of, wc, -ws)], 1).reshape(64, 512)
    v2 = np.stack([np.where(ri_of, wc, -ws), np.where(ri_of, -ws, -wc)], 1).reshape(64, 512)
    f0 = np.arange(LA)[:, None]
    sign = np.where((f0 >= LA // 2) & (ri_of[None] == 1), -1.0, 1.0)
    angle = 2.0 * math.pi / (LA * LB) * (f0 * j_of[None] % (LA * LB))
    cj, sj = np.cos(angle) * sign, np.sin(angle) * sign

    cos_c, sin_c = dft_tables(LC)
    lane = np.arange(128)
    k_of = 8 * (lane // 16) + lane % 8
    ri_of = lane // 8 % 2
    wc, ws = cos_c[:, k_of], sin_c[:, k_of]
    u3 = np.concatenate([np.where(ri_of, ws, wc), np.where(ri_of, wc, -ws)], 0)
    v3 = np.concatenate([np.where(ri_of, wc, -ws), np.where(ri_of, -ws, -wc)], 0)
    angle = 2.0 * math.pi / POINTS * (f0 * k_of[None] % POINTS)
    ca, sa = np.cos(angle), np.sin(angle)
    f1 = np.arange(LB)[:, None]
    angle = 2.0 * math.pi / (LB * LC) * (f1 * k_of[None] % (LB * LC))
    cb, sb = np.cos(angle), np.sin(angle)
    tables = (
        table_a, np.stack([table_lo, table_hi]), np.stack([u2, v2, cj, sj]),
        np.stack([u3, v3]), np.stack([ca, sa]), np.stack([cb, sb]),
    )
    return tuple(np.asarray(t, np.float32) for t in tables)


def kernel(
    tok_hbm, gain_hbm, win_hbm, skip_hbm, filt_hbm, wout_hbm,
    ta_hbm, tinv_hbm, two_hbm, three_hbm, tca_hbm, tcb_hbm,
    outv,
    tok, gain, wmix, wgate, skip, filt, wout,
    ta, tinv, two, three, tca, tcb,
    mixed, gate, xrecv, first, yzrecv, mid, mid2, bsend, brecv, csend, crecv, gated,
    m1, mlo, mhi, t2, t2t, t3, t3t,
    lsem, ss, xr, yr, br, cr,
):
    a = lax.axis_index("aa")
    b = lax.axis_index("ba")
    c = lax.axis_index("col")
    s = b * NC + c

    def fetch(n, src, dst):
        pltpu.make_async_copy(src, dst, lsem.at[n]).start()

    def landed(sem, ref):
        pltpu.make_async_copy(ref, ref, sem).wait()

    fetch(0, gain_hbm, gain)
    for g in range(NG):
        fetch(1 + g, tok_hbm.at[:, pl.ds(16 * g, 16), :], tok.at[g])
    for cc in range(NCC):
        for q in range(NA):
            for half, base in enumerate((0, 2 * D)):
                fetch(
                    5 + cc,
                    win_hbm.at[:, pl.ds(base + 256 * q + 128 * cc, 128)],
                    wmix.at[cc, q, :, pl.ds(128 * half, 128)],
                )
    fetch(7, ta_hbm, ta)
    fetch(8, tinv_hbm, tinv)
    fetch(9, win_hbm.at[:, pl.ds(D, D)], wgate)
    fetch(10, two_hbm, two)
    fetch(11, three_hbm, three)
    fetch(12, tca_hbm, tca)
    fetch(13, tcb_hbm, tcb)
    for cc in range(NCC):
        fetch(14 + cc, filt_hbm.at[..., pl.ds(128 * cc, 128)], filt.at[cc])
    fetch(16, skip_hbm, skip)
    fetch(17, wout_hbm, wout)

    def x_device(d):
        return {"aa": lax.rem(a + d, NA), "ba": b, "col": c}

    bits = [lax.rem(c, 2), lax.rem(c // 2, 2), c // 4, lax.rem(b, 2), b // 2]

    def partner(d):
        picked = [1 - bit if d >> n & 1 else bit for n, bit in enumerate(bits)]
        return picked[3] + 2 * picked[4], picked[0] + 2 * picked[1] + 4 * picked[2]

    def yz_device(tb, tc):
        return {"aa": a, "ba": tb, "col": tc}

    barrier = pltpu.get_barrier_semaphore()
    for d in range(1, NA):
        pl.semaphore_signal(barrier, inc=1, device_id=x_device(d), device_id_type=MESH)

    for d in range(1, SLOTS):
        pl.semaphore_signal(barrier, inc=1, device_id=yz_device(*partner(d)), device_id_type=MESH)

    def x_copy(d, cc, g):
        to = lax.rem(a + d, NA)
        return pltpu.make_async_remote_copy(
            src_ref=mixed.at[to, cc, g], dst_ref=xrecv.at[cc, g, a],
            send_sem=ss.at[0], recv_sem=xr.at[cc, g],
            device_id=x_device(d), device_id_type=MESH,
        )

    def mix(cc, g):
        rows = tok[g].reshape(ROWS, D)
        for q in range(NA):
            both = jnp.dot(rows, wmix[cc, q], preferred_element_type=jnp.float32)
            mixed[q, cc, g] = (both[:, :128] * both[:, 128:]).astype(jnp.bfloat16)

    def mix_send(cc, g):
        for d in (2, 1, 3):
            x_copy(d, cc, g).start()
        xrecv[cc, g, a] = mixed[a, cc, g]

    landed(lsem.at[0], gain)
    for g in range(NG):
        landed(lsem.at[1 + g], tok.at[g])

        @pl.loop(0, 4)
        def _(part):
            view = tok.at[g, pl.ds(4 * part, 4)]
            block = view[...].astype(jnp.float32).reshape(64, D)
            scale = lax.rsqrt(jnp.mean(block * block, axis=-1, keepdims=True) + EPSILON)
            view[...] = (block * scale * gain[...]).astype(jnp.bfloat16).reshape(4, 16, D)

        if g == 0:
            landed(lsem.at[5], wmix.at[0])
        mix(0, g)
        if g == 0:
            pl.semaphore_wait(barrier, NA - 1 + SLOTS - 1)
        mix_send(0, g)

    landed(lsem.at[7], ta)
    lane16 = lax.broadcasted_iota(jnp.int32, (16, 1024), 1)
    sub16 = lax.broadcasted_iota(jnp.int32, (16, 1024), 0)
    on16 = lax.rem(lane16, 16) == sub16

    @pl.loop(0, 2 * HALF)
    def _(r):
        m1[pl.ds(pl.multiple_of(16 * r, 16), 16), :] = jnp.where(on16, ta[pl.ds(r, 1), :], 0.0).astype(jnp.bfloat16)

    landed(lsem.at[6], wmix.at[1])

    def y_copy(d, cc, g):
        tb, tc = partner(d)
        t = tb * NC + tc
        p0 = jnp.where(t < SLOTS // 2, 2 * t, LA - 1 - 2 * t)
        return pltpu.make_async_remote_copy(
            src_ref=first.at[cc, g, pl.ds(p0, 2)], dst_ref=yzrecv.at[cc, :, c, b, g],
            send_sem=ss.at[1], recv_sem=yr.at[cc, g],
            device_id=yz_device(tb, tc), device_id_type=MESH,
        )

    own0 = jnp.where(s < SLOTS // 2, 2 * s, LA - 1 - 2 * s)

    @pl.loop(0, CHUNKS)
    def _(n):
        cc, g = n // NG, lax.rem(n, NG)
        landed(xr.at[cc, g], xrecv.at[cc, g, pl.ds(0, NA - 1)])
        value = jnp.dot(m1[...], xrecv[cc, g].reshape(1024, LANES), preferred_element_type=jnp.float32)
        first[cc, g] = value.astype(jnp.bfloat16).reshape(HALF, 32, LANES)

        for d in range(1, SLOTS):
            y_copy(d, cc, g).start()

        yzrecv[cc, :, c, b, g] = first[cc, g, pl.ds(own0, 2)]

        @pl.when(n < NG)
        def _():
            mix(1, n)
            mix_send(1, n)

    landed(lsem.at[9], wgate)

    @pl.loop(0, NG)
    def _(g):
        value = jnp.dot(tok[g].reshape(ROWS, D), wgate[...], preferred_element_type=jnp.float32)
        gate[g] = value.astype(jnp.bfloat16)

    landed(lsem.at[10], two)
    landed(lsem.at[11], three)
    landed(lsem.at[12], tca)
    landed(lsem.at[13], tcb)
    for cc in range(NCC):
        landed(lsem.at[14 + cc], filt.at[cc])
    landed(lsem.at[8], tinv)

    @pl.loop(0, LA)
    def _(r):
        at = pl.ds(pl.multiple_of(16 * r, 16), 16)
        mlo[at, :] = jnp.where(on16, tinv[0, pl.ds(r, 1), :], 0.0).astype(jnp.bfloat16)
        mhi[at, :] = jnp.where(on16, tinv[1, pl.ds(r, 1), :], 0.0).astype(jnp.bfloat16)

    lane8 = lax.broadcasted_iota(jnp.int32, (16, 512), 1)
    sub8 = lax.broadcasted_iota(jnp.int32, (16, 512), 0)
    on8 = lax.rem(lane8, 8) == lax.rem(sub8, 8)
    for u in range(2):
        f0 = jnp.where(s < SLOTS // 2, 2 * s + u, 2 * s + 1 - u)
        at0 = pl.ds(f0, 1)

        @pl.loop(0, LB)
        def _(f1):
            row0, row1 = pl.ds(2 * f1, 1), pl.ds(2 * f1 + 1, 1)
            up = two[0, row0, :] * two[2, at0, :] + two[1, row0, :] * two[3, at0, :]
            low = two[0, row1, :] * two[2, at0, :] + two[1, row1, :] * two[3, at0, :]
            value = jnp.where(on8, jnp.where(sub8 < 8, up, low), 0.0)
            t2[u, pl.ds(pl.multiple_of(16 * f1, 16), 16), :] = value.astype(jnp.bfloat16)

        @pl.loop(0, 4)
        def _(r):
            at = pl.ds(pl.multiple_of(128 * r, 128), 128)
            t2t[u, :, at] = jnp.transpose(t2[u, at, :].astype(jnp.float32)).astype(jnp.bfloat16)

        @pl.loop(0, LB)
        def _(f1):
            row = pl.ds(f1, 1)
            ec = tca[0, at0, :] * tcb[0, row, :] - tca[1, at0, :] * tcb[1, row, :]
            es = tca[1, at0, :] * tcb[0, row, :] + tca[0, at0, :] * tcb[1, row, :]
            value = three[0] * ec + three[1] * es
            t3[u, f1] = value.astype(jnp.bfloat16)
            t3t[u, f1] = jnp.transpose(value).astype(jnp.bfloat16)

    place = jnp.where(s < SLOTS // 2, 2 * s, 32 + 2 * (SLOTS - 1 - s))

    def b_copy(d, cc, g):
        tb, tc = partner(d)
        return pltpu.make_async_remote_copy(
            src_ref=bsend.at[cc, :, tc, tb, g], dst_ref=brecv.at[cc, g, pl.ds(place, 2)],
            send_sem=ss.at[2], recv_sem=br.at[cc, g],
            device_id=yz_device(tb, tc), device_id_type=MESH,
        )


    @pl.loop(0, NCC)
    def _(cc):
        for g in range(NG):
            landed(yr.at[cc, g], brecv.at[cc, g, pl.ds(0, 2 * (SLOTS - 1))])

        @pl.loop(0, 2)
        def _(u):
            l = jnp.where(s < SLOTS // 2, u, 1 - u)

            @pl.loop(0, NC // 2)
            def _(n):
                pair = [yzrecv[cc, u, 2 * n + m].reshape(512, LANES) for m in range(2)]
                value = jnp.dot(t2[u], jnp.concatenate(pair, axis=1), preferred_element_type=jnp.float32)
                value = value.astype(jnp.bfloat16)
                for m in range(2):
                    mid[:, 2 * n + m] = value[:, 128 * m : 128 * (m + 1)].reshape(LB, 16, LANES)

            @pl.loop(0, LB // 4)
            def _(n):
                spectra = []
                for e in range(4):
                    f1 = 4 * n + e
                    spectra.append(
                        jnp.dot(t3[u, f1], mid[f1].reshape(128, LANES), preferred_element_type=jnp.float32)
                    )
                outs = []
                for e in range(4):
                    f1 = 4 * n + e
                    xr_, xi_ = spectra[e][:64], spectra[e][64:]
                    hr = filt[cc, 0, l, f1].astype(jnp.float32)
                    hi = filt[cc, 1, l, f1].astype(jnp.float32)
                    outs.append(
                        jnp.concatenate([hr * xr_ - hi * xi_, hr * xi_ + hi * xr_], axis=0).astype(jnp.bfloat16)
                    )
                for e in range(4):
                    f1 = 4 * n + e
                    value = jnp.dot(t3t[u, f1], outs[e], preferred_element_type=jnp.float32)
                    mid2[f1] = value.astype(jnp.bfloat16).reshape(NC, 16, LANES)

            @pl.loop(0, NC // 2)
            def _(n):
                pair = [mid2[:, 2 * n + m].reshape(512, LANES) for m in range(2)]
                value = jnp.dot(t2t[u], jnp.concatenate(pair, axis=1), preferred_element_type=jnp.float32)
                value = value.astype(jnp.bfloat16)
                for m in range(2):
                    bsend[cc, u, 2 * n + m] = value[:, 128 * m : 128 * (m + 1)].reshape(NB, NG, 32, LANES)

        @pl.loop(0, NG)
        def _(g):
            for d in range(1, SLOTS):
                b_copy(d, cc, g).start()

            brecv[cc, g, pl.ds(place, 2)] = bsend[cc, :, c, b, g]

    def c_copy(d, cc, g):
        to = lax.rem(a + d, NA)
        return pltpu.make_async_remote_copy(
            src_ref=csend.at[cc, g, to], dst_ref=crecv.at[cc, g, a],
            send_sem=ss.at[3], recv_sem=cr.at[cc, g],
            device_id=x_device(d), device_id_type=MESH,
        )

    landed(lsem.at[16], skip)
    landed(lsem.at[17], wout)

    @pl.loop(0, CHUNKS)
    def _(n):
        cc, g = n // NG, lax.rem(n, NG)

        landed(br.at[cc, g], brecv.at[cc, g, pl.ds(0, 2 * (SLOTS - 1))])
        low = brecv[cc, g, pl.ds(0, 32)].reshape(1024, LANES)
        high = brecv[cc, g, pl.ds(32, 32)].reshape(1024, LANES)
        value = jnp.dot(mlo[...], low, preferred_element_type=jnp.float32)
        value += jnp.dot(mhi[...], high, preferred_element_type=jnp.float32)
        csend[cc, g] = value.astype(jnp.bfloat16).reshape(NA, ROWS, LANES)
        for d in (2, 1, 3):
            c_copy(d, cc, g).start()
        crecv[cc, g, a] = csend[cc, g, a]

    for g in range(NG):
        for cc in range(NCC):
            landed(cr.at[cc, g], crecv.at[cc, g, pl.ds(0, NA - 1)])
        for q in range(NA):
            for cc in range(NCC):
                at = pl.ds(256 * q + 128 * cc, 128)
                conv = crecv[cc, g, q].astype(jnp.float32)
                plus = conv + skip[:, at] * mixed[q, cc, g].astype(jnp.float32)
                gated[:, at] = (gate[g, :, at].astype(jnp.float32) * plus).astype(jnp.bfloat16)
        value = jnp.dot(gated[...], wout[...], preferred_element_type=jnp.float32)
        outv[:, 16 * g : 16 * (g + 1), :] = value.astype(jnp.bfloat16).reshape(16, 16, D)

    for cc in range(NCC):
        for g in range(NG):
            landed(ss.at[0], xrecv.at[cc, g, pl.ds(0, NA - 1)])
            landed(ss.at[1], brecv.at[cc, g, pl.ds(0, 2 * (SLOTS - 1))])
            landed(ss.at[2], brecv.at[cc, g, pl.ds(0, 2 * (SLOTS - 1))])
            landed(ss.at[3], crecv.at[cc, g, pl.ds(0, NA - 1)])


def local(tokens, norm_gain, in_weight, skip_gain, spectrum_filter, out_weight):
    tables = [jnp.asarray(t) for t in static_tables()]
    bf, f32 = jnp.bfloat16, jnp.float32
    vmem = pltpu.VMEM
    dma = pltpu.SemaphoreType.DMA
    scratch = [
        vmem((NG, 16, 16, D), bf), vmem((1, D), f32), vmem((NCC, NA, D, 256), bf), vmem((D, D), bf),
        vmem((1, D), f32), vmem((NCC, 2, 2, LB, LC, LANES), bf), vmem((D, D), bf),
        *[vmem(t.shape, f32) for t in tables],
        vmem((NA, NCC, NG, ROWS, LANES), bf),
        vmem((NG, ROWS, D), bf),
        vmem((NCC, NG, NA, ROWS, LANES), bf),
        vmem((NCC, NG, HALF, 32, LANES), bf),
        vmem((NCC, 2, NC, NB, NG, 32, LANES), bf),
        vmem((LB, NC, 16, LANES), bf),
        vmem((LB, NC, 16, LANES), bf),
        vmem((NCC, 2, NC, NB, NG, 32, LANES), bf),
        vmem((NCC, NG, 64, 32, LANES), bf),
        vmem((NCC, NG, NA, ROWS, LANES), bf),
        vmem((NCC, NG, NA, ROWS, LANES), bf),
        vmem((ROWS, D), bf),
        vmem((HALF * 32, 1024), bf), vmem((1024, 1024), bf), vmem((1024, 1024), bf),
        vmem((2, 512, 512), bf), vmem((2, 512, 512), bf),
        vmem((2, LB, 128, 128), bf), vmem((2, LB, 128, 128), bf),
        dma((18,)), dma((4,)), dma((NCC, NG)), dma((NCC, NG)), dma((NCC, NG)), dma((NCC, NG)),
    ]
    out = pl.pallas_call(
        kernel,
        out_shape=jax.ShapeDtypeStruct((16, 64, D), bf),
        in_specs=[pl.BlockSpec(memory_space=pl.ANY)] * (6 + len(tables)),
        out_specs=pl.BlockSpec(memory_space=pltpu.VMEM),
        scratch_shapes=scratch,
        compiler_params=pltpu.CompilerParams(
            collective_id=0, has_side_effects=True, vmem_limit_bytes=67043328
        ),
    )(
        tokens.reshape(16, 64, D), norm_gain.reshape(1, D), in_weight, skip_gain.reshape(1, D),
        spectrum_filter, out_weight, *tables,
    )
    return out.reshape(16, 8, 8, D)


def solution(mesh):
    in_specs = (
        P("aa", "ba", "col", None),
        P(),
        P(),
        P(),
        P(None, ("ba", "col"), None, None, "aa"),
        P(),
    )
    out_specs = P("aa", "ba", "col", None)
    return jax.shard_map(local, mesh=mesh, in_specs=in_specs, out_specs=out_specs, check_vma=False)
```

time: 146 us -> 121 us (0.83)
  Pallas kernels: 143 us -> 117 us
    pallas_call x1, Pallas kernels: 143 us -> 117 us  [local(): pl.pallas_call(kernel, out_shape=jax.ShapeDtypeStruct((16, 64, D), bf), i...]
where the time goes in v1:
time: 121 us; the launch traced here: 120 us
  Pallas kernels  117 us (97%)
  local copies, waits for them, and re-layouts  3.14 us (3%)
    pallas_call x1, Pallas kernels, local(): pl.pallas_call(kernel, out_shape=jax.ShapeDtypeStruct((16, 64, D), bf), i...  117 us
    unnamed x1, local copies, waits for them, and re-layouts  3.14 us

profile of v1, /device:TPU:1, one launch (start us, length us, event | category | flops | bytes accessed | tf_op | source)
XLA Modules:
  0.0 120.2 jit_solution(12061716622778650727)
XLA Ops:
  0.0 117.0 %shard_map.118 = bf16[16,64,1024]{2,1,0:T(8,128)(2,1)} custom-call(bf16[16,64,1024]{2,1,0:T(8,128)(2,1)} %bitcast.5, f32[1,1024]{1,0:T(1,128)} %bitcast.6, bf16[1024,3072]{1,0:T(8,128)(2,1)} %win_hbm.1, f32[1,1024]{1,0:T(1,128)} %bitcast.7, bf16[2,2,32,64,256]{4,3,2,1,0:T(8,128)(2,1)} %filt_hbm.1, bf16[1024,1024]{1,0:T(8,128)(2,1)} %wout_hbm.1, ...), custom_call_target="tpu_custom_call" | custom-call | tf_op jit(solution)/shard_map/pallas_call | solution.py:407
  117.0 3.1 %copy.14 = bf16[16,8,8,1024]{3,2,1,0:T(8,128)(2,1)} copy(bf16[16,8,8,1024]{3,2,1,0:T(8,128)(2,1)} %bitcast.4) | data formatting | bytes 4194304

commit v2 on v1

--- a/solution.py
+++ b/solution.py
@@ -99,31 +99,40 @@
     def landed(sem, ref):
         pltpu.make_async_copy(ref, ref, sem).wait()
 
-    fetch(0, gain_hbm, gain)
-    for g in range(NG):
-        fetch(1 + g, tok_hbm.at[:, pl.ds(16 * g, 16), :], tok.at[g])
-    for cc in range(NCC):
+    def fetch_mix(cc):
         for q in range(NA):
             for half, base in enumerate((0, 2 * D)):
-                fetch(
-                    5 + cc,
-                    win_hbm.at[:, pl.ds(base + 256 * q + 128 * cc, 128)],
-                    wmix.at[cc, q, :, pl.ds(128 * half, 128)],
-                )
+                at = pl.ds(base + 256 * q + 128 * cc, 128)
+                fetch(5 + cc, win_hbm.at[:, at], wmix.at[cc, q, :, pl.ds(128 * half, 128)])
+
+    fetch(0, gain_hbm, gain)
+    fetch(1, tok_hbm.at[:, pl.ds(0, 16), :], tok.at[0])
+    fetch_mix(0)
     fetch(7, ta_hbm, ta)
-    fetch(8, tinv_hbm, tinv)
-    fetch(9, win_hbm.at[:, pl.ds(D, D)], wgate)
-    fetch(10, two_hbm, two)
-    fetch(11, three_hbm, three)
-    fetch(12, tca_hbm, tca)
-    fetch(13, tcb_hbm, tcb)
-    for cc in range(NCC):
-        fetch(14 + cc, filt_hbm.at[..., pl.ds(128 * cc, 128)], filt.at[cc])
-    fetch(16, skip_hbm, skip)
-    fetch(17, wout_hbm, wout)
+
+    def fetch_rest():
+        for g in range(1, NG):
+            fetch(1 + g, tok_hbm.at[:, pl.ds(16 * g, 16), :], tok.at[g])
+        fetch_mix(1)
+        fetch(9, win_hbm.at[:, pl.ds(D, D)], wgate)
+        fetch(8, tinv_hbm, tinv)
+        fetch(10, two_hbm, two)
+        fetch(11, three_hbm, three)
+        fetch(12, tca_hbm, tca)
+        fetch(13, tcb_hbm, tcb)
+        for cc in range(NCC):
+            fetch(14 + cc, filt_hbm.at[..., pl.ds(128 * cc, 128)], filt.at[cc])
+        fetch(16, skip_hbm, skip)
+        fetch(17, wout_hbm, wout)
+
+    x_bits = [lax.rem(a, 2), a // 2]
+
+    def x_index(d):
+        picked = [1 - bit if d >> n & 1 else bit for n, bit in enumerate(x_bits)]
+        return picked[0] + 2 * picked[1]
 
     def x_device(d):
-        return {"aa": lax.rem(a + d, NA), "ba": b, "col": c}
+        return {"aa": x_index(d), "ba": b, "col": c}
 
     bits = [lax.rem(c, 2), lax.rem(c // 2, 2), c // 4, lax.rem(b, 2), b // 2]
 
@@ -142,7 +151,7 @@
         pl.semaphore_signal(barrier, inc=1, device_id=yz_device(*partner(d)), device_id_type=MESH)
 
     def x_copy(d, cc, g):
-        to = lax.rem(a + d, NA)
+        to = x_index(d)
         return pltpu.make_async_remote_copy(
             src_ref=mixed.at[to, cc, g], dst_ref=xrecv.at[cc, g, a],
             send_sem=ss.at[0], recv_sem=xr.at[cc, g],
@@ -173,6 +182,8 @@
 
         if g == 0:
             landed(lsem.at[5], wmix.at[0])
+        if g == 0:
+            fetch_rest()
         mix(0, g)
         if g == 0:
             pl.semaphore_wait(barrier, NA - 1 + SLOTS - 1)
@@ -334,7 +345,7 @@
             brecv[cc, g, pl.ds(place, 2)] = bsend[cc, :, c, b, g]
 
     def c_copy(d, cc, g):
-        to = lax.rem(a + d, NA)
+        to = x_index(d)
         return pltpu.make_async_remote_copy(
             src_ref=csend.at[cc, g, to], dst_ref=crecv.at[cc, g, a],
             send_sem=ss.at[3], recv_sem=cr.at[cc, g],
@@ -406,12 +417,12 @@
     ]
     out = pl.pallas_call(
         kernel,
-        out_shape=jax.ShapeDtypeStruct((16, 64, D), bf),
-        in_specs=[pl.BlockSpec(memory_space=pl.ANY)] * (6 + len(tables)),
+        out_shape=pltpu.VMEM((16, 64, D), bf),
+        in_specs=[pl.BlockSpec(memory_space=pltpu.HBM)] * (6 + len(tables)),
         out_specs=pl.BlockSpec(memory_space=pltpu.VMEM),
         scratch_shapes=scratch,
         compiler_params=pltpu.CompilerParams(
-            collective_id=0, has_side_effects=True, vmem_limit_bytes=67043328
+            collective_id=0, has_side_effects=True, vmem_limit_bytes=58*2**20
         ),
     )(
         tokens.reshape(16, 64, D), norm_gain.reshape(1, D), in_weight, skip_gain.reshape(1, D),

time: 121 us -> 118 us (0.975)
  local copies, waits for them, and re-layouts: 3.14 us -> 1.32 us
    unnamed x1, local copies, waits for them, and re-layouts: 3.14 us -> 1.32 us
    pallas_call x1, Pallas kernels: 117 us -> 116 us  [local(): pl.pallas_call(kernel, out_shape=pltpu.VMEM((16, 64, D), bf), in_specs=[p...]
where the time goes in v2:
time: 118 us; the launch traced here: 117 us
  Pallas kernels  116 us (98%)
  local copies, waits for them, and re-layouts  1.32 us (1%)
    pallas_call x1, Pallas kernels, local(): pl.pallas_call(kernel, out_shape=pltpu.VMEM((16, 64, D), bf), in_specs=[p...  116 us

profile of v2, /device:TPU:1, one launch (start us, length us, event | category | flops | bytes accessed | tf_op | source)
XLA Modules:
  0.0 116.9 jit_solution(14199764405607562185)
XLA Ops:
  0.0 115.6 %shard_map.118 = bf16[16,64,1024]{2,1,0:T(8,128)(2,1)S(1)} custom-call(bf16[16,64,1024]{2,1,0:T(8,128)(2,1)} %bitcast.5, f32[1,1024]{1,0:T(1,128)} %bitcast.6, bf16[1024,3072]{1,0:T(8,128)(2,1)} %win_hbm.1, f32[1,1024]{1,0:T(1,128)} %bitcast.7, bf16[2,2,32,64,256]{4,3,2,1,0:T(8,128)(2,1)} %filt_hbm.1, bf16[1024,1024]{1,0:T(8,128)(2,1)} %wout_hbm.1, ...), custom_call_target="tpu_custom_call" | custom-call | tf_op jit(solution)/shard_map/pallas_call | solution.py:418
  115.6 1.3 %copy.14 = bf16[16,8,8,1024]{3,2,1,0:T(8,128)(2,1)} copy(bf16[16,8,8,1024]{3,2,1,0:T(8,128)(2,1)S(1)} %bitcast.4) | data formatting | bytes 4194304
